TPU v7x, 32 devices: a whole 2x2x4 slice. The times are simulated.
32 devices in a mesh: rep: 4 (over y, x), shard: 8 (over z, core).
Axes of the slice: x: 2, y: 2, z: 4, core: 2. Of those that a mesh axis runs over, the one named last changes fastest.
Arguments:
- hot_ids: int32 [65536], P(('rep', 'shard')), may hold values from 0 to 8191
- hot_grads: bfloat16 [65536, 128], P(('rep', 'shard')), may hold values from -6 to 6
- hot_rows: float32 [8192, 128], replicated, may hold values from -6 to 6
- hot_accum: float32 [8192], replicated, may hold values from 0.5 to 4
- cold_counts: int32 [32, 32], P(('rep', 'shard')), may hold values from 1 to 16, as said below
- cold_slots: int32 [32, 32, 16], P(('rep', 'shard')), may hold values from 0 to 8191
- cold_grads: bfloat16 [32, 32, 16, 128], P(('rep', 'shard')), may hold values from -6 to 6
- cold_rows: float32 [262144, 128], P(('rep', 'shard')), may hold values from -6 to 6
- cold_accum: float32 [262144], P(('rep', 'shard')), may hold values from 0.5 to 4
Outputs:
- new_hot_rows: float32 [8192, 128], replicated
- new_hot_accum: float32 [8192], replicated
- new_cold_rows: float32 [262144, 128], P(('rep', 'shard'))
- new_cold_accum: float32 [262144], P(('rep', 'shard'))
Inputs may be any that keep to these rules, and one draw needn't show every extreme that they name: `cold_counts`: every entry is at least 1 and at most 16; in every draw some owner receives 16 live slots from every sender.
All inputs are finite; a program needn't handle non-finite values.
Results may differ from a plain program's by a relative error of at most 0.0003.
Values may be sent and summed in bfloat16 or wider, within the bound.
A program may use at most 128 MiB of HBM per device.

v0:
```python
import jax
import jax.numpy as jnp
from jax import lax
from jax.sharding import PartitionSpec as P

learn_rate = 0.5


def adagrad(table_rows, accum_rows, gradient):
    accum_new = accum_rows + jnp.mean(gradient * gradient, axis=1)
    return (table_rows - learn_rate * gradient / jnp.sqrt(accum_new)[:, None], accum_new)


def local(
    hot_ids,
    hot_grads,
    hot_rows,
    hot_accum,
    cold_counts,
    cold_slots,
    cold_grads,
    cold_rows,
    cold_accum,
):
    hot_count = hot_rows.shape[0]
    dense = jax.ops.segment_sum(hot_grads.astype(jnp.float32), hot_ids, num_segments=hot_count)
    share = hot_count // lax.axis_size("shard")
    part_sum = lax.psum_scatter(dense, "shard", scatter_dimension=0, tiled=True)
    part_sum = lax.psum(part_sum, "rep")
    start = lax.axis_index("shard") * share
    rows_share = lax.dynamic_slice_in_dim(hot_rows, start, share, 0)
    accum_share = lax.dynamic_slice_in_dim(hot_accum, start, share, 0)
    rows_new, accum_new = adagrad(rows_share, accum_share, part_sum)
    new_hot_rows, new_hot_accum = (
        lax.all_gather(rows_new, "shard", axis=0, tiled=True),
        lax.all_gather(accum_new, "shard", axis=0, tiled=True),
    )
    received, slots_in, counts_in = (
        lax.all_to_all(cold_grads, ("rep", "shard"), split_axis=1, concat_axis=0, tiled=True),
        lax.all_to_all(cold_slots, ("rep", "shard"), split_axis=1, concat_axis=0, tiled=True),
        lax.all_to_all(cold_counts, ("rep", "shard"), split_axis=1, concat_axis=0, tiled=True),
    )
    width = received.shape[-1]
    capacity = received.shape[2]
    slot_index = lax.broadcasted_iota(jnp.int32, (1, 1, capacity), 2)
    live_mask = slot_index < counts_in[:, :, None]
    masked_terms = jnp.where(live_mask[..., None], received.astype(jnp.float32), 0.0)
    local_rows = cold_rows.shape[0]
    cold_sum = jax.ops.segment_sum(
        masked_terms.reshape(-1, width), slots_in.reshape(-1), num_segments=local_rows
    )
    new_cold_rows, new_cold_accum = adagrad(cold_rows, cold_accum, cold_sum)
    return (new_hot_rows, new_hot_accum, new_cold_rows, new_cold_accum)


def solution(mesh):
    placed = (
        P(("rep", "shard")),
        P(("rep", "shard"), None),
        P(),
        P(),
        P(("rep", "shard"), None),
        P(("rep", "shard"), None, None),
        P(("rep", "shard"), None, None, None),
        P(("rep", "shard"), None),
        P(("rep", "shard")),
    )
    return jax.shard_map(
        local,
        mesh=mesh,
        in_specs=placed,
        out_specs=(P(), P(), P(("rep", "shard"), None), P(("rep", "shard"))),
        check_vma=False,
    )
```

profile of v0, /device:TPU:0, one launch (start us, length us, event | category | flops | bytes accessed | tf_op | source)
XLA Modules:
  0.0 199.6 jit_solution(5830766798041887270)
XLA Ops:
  7.2 14.1 %scatter_custom_fusion = f32[8192,128]{1,0:T(8,128)} fusion(s32[2048]{0:T(1024)} %param.9, f32[]{:T(128)} %constant.3.clone.1, bf16[2048,128]{1,0:T(8,128)(2,1)} %param.10), kind=kCustom, calls=%fused_computation.6 | custom fusion | flops 524288 | bytes 4719104 | tf_op jit(solution)/shard_map/scatter-add | solution.py:26
  21.4 52.8 %reduce-scatter.2.cloned.1.call-done = f32[1024,128]{1,0:T(8,128)} async-done(((f32[8192,128]{1,0:T(8,128)}), f32[1024,128]{1,0:T(8,128)}) %reduce-scatter.2.cloned.1.call-update) | async-done | bytes 524304 | tf_op jit(solution)/shard_map/reduce_scatter | solution.py:28
  74.2 46.8 %all-reduce.2.cloned.1.call-done = f32[1024,128]{1,0:T(8,128)} async-done(((f32[1024,128]{1,0:T(8,128)}), f32[1024,128]{1,0:T(8,128)}) %all-reduce.2.cloned.1.call-update) | async-done | bytes 524304 | tf_op jit(solution)/shard_map/psum | solution.py:29
  121.0 1.2 multiply_reduce_fusion.1
  122.2 0.7 fusion.8
  122.9 2.2 %divide_subtract_fusion.1 = f32[1024,128]{1,0:T(8,128)} fusion(f32[1024,128]{1,0:T(8,128)} %all-reduce.2.cloned.1.call-done, f32[8192,128]{1,0:T(8,128)} %param.11, s32[]{:T(128)S(6)} %select_n.11, f32[1024]{0:T(1024)S(1)} %get-tuple-element.6), kind=kLoop, calls=%fused_computation.9 | loop fusion | flops 393216 | bytes 1576964 | tf_op jit(solution)/shard_map/sub | solution.py:11
  125.2 0.7 copy.18
  125.9 4.6 %all-to-all-start.1 = ((s32[1,32,1]{2,0,1:T(1,128)}), s32[1,32,1]{2,0,1:T(1,128)S(1)}, u32[]{:S(2)}, u32[]{:S(2)}) async-start(s32[1,32,1]{2,0,1:T(1,128)} %copy.18), calls=%async_computation.2 | async-start | bytes 32768 | tf_op jit(solution)/shard_map/all_to_all | solution.py:41
  130.6 7.0 %all-to-all-done.1 = s32[1,32,1]{2,0,1:T(1,128)S(1)} async-done(((s32[1,32,1]{2,0,1:T(1,128)}), s32[1,32,1]{2,0,1:T(1,128)S(1)}, u32[]{:S(2)}, u32[]{:S(2)}) %all-to-all-start.1) | async-done | bytes 160 | tf_op jit(solution)/shard_map/all_to_all | solution.py:41
  137.6 9.1 %all_to_all.31 = s32[1,32,16]{2,0,1:T(1,128)S(1)} all-to-all(s32[1,32,16]{2,0,1:T(1,128)S(1)} %copy.17), channel_id=1, replica_groups=mesh['rep'=4,'shard'=8] {'rep','shard'}, dimensions={1} | all-to-all | bytes 4096 | tf_op jit(solution)/shard_map/all_to_all | solution.py:40
  146.7 2.6 %all-to-all-start.2 = ((bf16[1,32,16,128]{3,2,0,1:T(8,128)(2,1)}), bf16[1,32,16,128]{3,2,0,1:T(8,128)(2,1)S(1)}, u32[]{:S(2)}, u32[]{:S(2)}) async-start(bf16[1,32,16,128]{3,2,0,1:T(8,128)(2,1)} %bitcast.1), calls=%async_computation.3 | async-start | bytes 262144 | tf_op jit(solution)/shard_map/all_to_all | solution.py:39
  149.3 0.7 reduce.1
  150.0 0.1 lt.33
  150.1 0.5 broadcast.40
  150.6 0.7 reduce.4
  151.3 0.1 reshape.77
  151.4 9.5 %all-to-all-done.2 = bf16[1,32,16,128]{3,2,0,1:T(8,128)(2,1)S(1)} async-done(((bf16[1,32,16,128]{3,2,0,1:T(8,128)(2,1)}), bf16[1,32,16,128]{3,2,0,1:T(8,128)(2,1)S(1)}, u32[]{:S(2)}, u32[]{:S(2)}) %all-to-all-start.2) | async-done | bytes 131104 | tf_op jit(solution)/shard_map/all_to_all | solution.py:39
  160.9 4.6 %scatter_custom_fusion.1 = f32[8192,128]{1,0:T(8,128)} fusion(s32[512]{0:T(512)S(1)} %reshape.77, f32[]{:T(128)} %constant.3.clone.1, bf16[512,128]{1,0:T(8,128)(2,1)S(1)} %bitcast.7, pred[512]{0:T(512)(128)(4,1)S(1)} %lt.33), kind=kCustom, calls=%fused_computation.4 | custom fusion | flops 196608 | bytes 4326912 | tf_op jit(solution)/shard_map/scatter-add | solution.py:49
  165.5 3.5 %multiply_reduce_fusion = f32[8192]{0:T(1024)S(1)} fusion(f32[8192,128]{1,0:T(8,128)} %scatter_custom_fusion.1), kind=kLoop, calls=%fused_computation.3 | loop fusion | flops 2088960 | bytes 4227072 | tf_op jit(solution)/shard_map/reduce_sum | solution.py:10
  169.1 0.6 fusion.7
  169.7 4.2 %divide_subtract_fusion = f32[8192,128]{1,0:T(8,128)} fusion(f32[8192,128]{1,0:T(8,128)} %param.16, f32[8192,128]{1,0:T(8,128)S(1)} %copy-done, f32[8192]{0:T(1024)S(1)} %get-tuple-element.4), kind=kLoop, calls=%fused_computation.2 | loop fusion | flops 3145728 | bytes 12615680 | tf_op jit(solution)/shard_map/sub | solution.py:11
  173.9 14.1 %all_gather.7 = f32[8192]{0:T(1024)S(1)} all-gather(f32[1024]{0:T(1024)S(1)} %get-tuple-element.7), channel_id=1, replica_groups=mesh['rep'=4,'shard'=8] {'shard'}, dimensions={0}, use_global_device_ids=true | all-gather | bytes 36864 | tf_op jit(solution)/shard_map/all_gather | solution.py:36
  188.0 4.5 %copy.23 = f32[8192,128]{1,0:T(8,128)} copy(f32[8192,128]{1,0:T(8,128)} %all-gather.2.cloned.1.call-done) | data formatting | bytes 8388608
  192.4 0.6 copy.24
  (17 shorter events, 0.3 us)
Async XLA Ops:
  7.2 67.0 %reduce-scatter.2.cloned.1.call-start = ((), (), s32[]{:S(2)}) async-start(), calls=%async_computation.4 | async-start | bytes 4718592 | tf_op jit(solution)/shard_map/reduce_scatter | solution.py:28
  21.3 103.9 %copy-start.3 = (s32[1,32]{1,0:T(1,128)S(1)}, s32[1,32]{1,0:T(1,128)}, u32[]{:S(2)}) copy-start(s32[1,32]{1,0:T(1,128)} %param.13) | copy-start | bytes 388
  21.3 109.2 %copy-start.2 = (s32[1,32,16]{1,2,0:T(8,128)S(1)}, s32[1,32,16]{1,2,0:T(8,128)}, u32[]{:S(2)}) copy-start(s32[1,32,16]{1,2,0:T(8,128)} %param.14) | copy-start | bytes 6148
  21.3 99.7 %all-reduce.2.cloned.1.call-start = ((), (), s32[]{:S(2)}) async-start(), calls=%async_computation.5 | async-start | bytes 1048576 | tf_op jit(solution)/shard_map/psum | solution.py:29
  74.2 113.8 %all-gather.2.cloned.1.call-start = ((), (), s32[]{:S(2)}) async-start(), calls=%async_computation.6 | async-start | bytes 4718592 | tf_op jit(solution)/shard_map/all_gather | solution.py:35
  125.9 11.7 %all-to-all-start.1 = ((s32[1,32,1]{2,0,1:T(1,128)}), s32[1,32,1]{2,0,1:T(1,128)S(1)}, u32[]{:S(2)}, u32[]{:S(2)}) async-start(s32[1,32,1]{2,0,1:T(1,128)} %copy.18), calls=%async_computation.2 | async-start | bytes 32768 | tf_op jit(solution)/shard_map/all_to_all | solution.py:41
  146.7 14.2 %all-to-all-start.2 = ((bf16[1,32,16,128]{3,2,0,1:T(8,128)(2,1)}), bf16[1,32,16,128]{3,2,0,1:T(8,128)(2,1)S(1)}, u32[]{:S(2)}, u32[]{:S(2)}) async-start(bf16[1,32,16,128]{3,2,0,1:T(8,128)(2,1)} %bitcast.1), calls=%async_computation.3 | async-start | bytes 262144 | tf_op jit(solution)/shard_map/all_to_all | solution.py:39
  160.9 8.1 %copy-start.1 = (f32[8192]{0:T(1024)S(1)}, f32[8192]{0:T(1024)}, u32[]{:S(2)}) copy-start(f32[8192]{0:T(1024)} %param.17) | copy-start | bytes 98308
  165.5 4.1 %copy-start = (f32[8192,128]{1,0:T(8,128)S(1)}, f32[8192,128]{1,0:T(8,128)}, u32[]{:S(2)}) copy-start(f32[8192,128]{1,0:T(8,128)} %scatter_custom_fusion.1) | copy-start | bytes 12582916
Sparse Core Ops, SparseCore 0:
  21.4 52.6 reduce-scatter.1
  77.1 43.8 all-reduce.1
  125.3 50.0 all-gather.1
where the time goes:
time: 200 us
  waiting for transfers between devices  116 us (58%)
  other arithmetic  32.6 us (16%)
  blocking collectives  23.2 us (12%)
  between operations  13.8 us (7%)
  starting transfers between devices  7.29 us (4%)
  local copies, waits for them, and re-layouts  6.56 us (3%)
    reduce_scatter x1, waiting for transfers between devices, local(): part_sum = lax.psum_scatter(dense, 'shard', scatter_dimension=0, tiled=True)  52.8 us
    psum x1, waiting for transfers between devices, local(): part_sum = lax.psum(part_sum, 'rep')  46.8 us
    scatter-add x1, other arithmetic, local(): jax.ops.segment_sum(hot_grads.astype(jnp.float32), hot_ids, num_segments=...  14.1 us
    all_gather x1, blocking collectives, local(): lax.all_gather(accum_new, 'shard', axis=0, tiled=True)  14.1 us
    all_to_all x1, waiting for transfers between devices, local(): lax.all_to_all(cold_grads, ('rep', 'shard'), split_axis=1, concat_axis=0,...  9.51 us
    all_to_all x1, blocking collectives, local(): lax.all_to_all(cold_slots, ('rep', 'shard'), split_axis=1, concat_axis=0,...  9.13 us
    all_to_all x1, waiting for transfers between devices, local(): lax.all_to_all(cold_counts, ('rep', 'shard'), split_axis=1, concat_axis=0...  7.01 us
    sub x2, other arithmetic, adagrad(): table_rows - learn_rate * gradient / jnp.sqrt(accum_new)[:, None]  6.43 us
  transfers between devices with their start and end apart: 5, of which 4 were waited for; matrix products, arithmetic and copies ran while one was open for 8% of the time, Pallas kernels for 0%

commit v1 on v0

--- a/solution.py
+++ b/solution.py
@@ -2,6 +2,7 @@
 import jax.numpy as jnp
 from jax import lax
 from jax.sharding import PartitionSpec as P
+from jax.lax import all_gather
 
 learn_rate = 0.5
 
@@ -26,7 +27,13 @@
     dense = jax.ops.segment_sum(hot_grads.astype(jnp.float32), hot_ids, num_segments=hot_count)
     share = hot_count // lax.axis_size("shard")
     part_sum = lax.psum_scatter(dense, "shard", scatter_dimension=0, tiled=True)
-    part_sum = lax.psum(part_sum, "rep")
+
+    def form_domain_all(local_values, group_axis):
+        z1 = all_gather(local_values, axis_name=group_axis)
+        upper = jnp.sum(z1, axis=0)
+        return upper
+
+    part_sum = form_domain_all(part_sum, "rep")
     start = lax.axis_index("shard") * share
     rows_share = lax.dynamic_slice_in_dim(hot_rows, start, share, 0)
     accum_share = lax.dynamic_slice_in_dim(hot_accum, start, share, 0)

time: 200 us -> 189 us (0.945)
  waiting for transfers between devices: 116 us -> 105 us
    psum x1 -> x0, waiting for transfers between devices: 46.8 us -> none  [local(): part_sum = lax.psum(part_sum, 'rep')]
    all_gather x0 -> x1, waiting for transfers between devices: none -> 35.4 us  [form_domain_all(): z1 = all_gather(local_values, axis_name=group_axis)]
where the time goes in v1:
time: 189 us
  waiting for transfers between devices  105 us (56%)
  other arithmetic  33.2 us (18%)
  blocking collectives  23.2 us (12%)
  between operations  13.8 us (7%)
  starting transfers between devices  7.29 us (4%)
  local copies, waits for them, and re-layouts  6.56 us (3%)
    reduce_scatter x1, waiting for transfers between devices, local(): part_sum = lax.psum_scatter(dense, 'shard', scatter_dimension=0, tiled=True)  52.8 us
    all_gather x1, waiting for transfers between devices, form_domain_all(): z1 = all_gather(local_values, axis_name=group_axis)  35.4 us
    scatter-add x1, other arithmetic, local(): jax.ops.segment_sum(hot_grads.astype(jnp.float32), hot_ids, num_segments=...  14.1 us
    all_gather x1, blocking collectives, local(): lax.all_gather(accum_new, 'shard', axis=0, tiled=True)  14.1 us
    all_to_all x1, waiting for transfers between devices, local(): lax.all_to_all(cold_grads, ('rep', 'shard'), split_axis=1, concat_axis=0,...  9.51 us
    all_to_all x1, blocking collectives, local(): lax.all_to_all(cold_slots, ('rep', 'shard'), split_axis=1, concat_axis=0,...  9.13 us
    all_to_all x1, waiting for transfers between devices, local(): lax.all_to_all(cold_counts, ('rep', 'shard'), split_axis=1, concat_axis=0...  7.02 us
    sub x2, other arithmetic, adagrad(): table_rows - learn_rate * gradient / jnp.sqrt(accum_new)[:, None]  6.27 us
  transfers between devices with their start and end apart: 5, of which 4 were waited for; matrix products, arithmetic and copies ran while one was open for 8% of the time, Pallas kernels for 0%

profile of v1, /device:TPU:0, one launch (start us, length us, event | category | flops | bytes accessed | tf_op | source)
XLA Modules:
  0.0 188.8 jit_solution(13003348099846185917)
XLA Ops:
  7.2 14.1 %scatter_custom_fusion = f32[8192,128]{1,0:T(8,128)} fusion(s32[2048]{0:T(1024)} %param.9, f32[]{:T(128)} %constant.3.clone.1, bf16[2048,128]{1,0:T(8,128)(2,1)} %param.10), kind=kCustom, calls=%fused_computation.6 | custom fusion | flops 524288 | bytes 4719104 | tf_op jit(solution)/shard_map/scatter-add | solution.py:27
  21.4 52.8 %reduce-scatter.2.cloned.1.call-done = f32[1024,128]{1,0:T(8,128)} async-done(((f32[8192,128]{1,0:T(8,128)}), f32[1024,128]{1,0:T(8,128)}) %reduce-scatter.2.cloned.1.call-update) | async-done | bytes 524304 | tf_op jit(solution)/shard_map/reduce_scatter | solution.py:29
  74.2 35.4 %all-gather.6.cloned.1.call-done = f32[4096,128]{1,0:T(8,128)} async-done(((f32[1024,128]{1,0:T(8,128)}), f32[4096,128]{1,0:T(8,128)}) %all-gather.6.cloned.1.call-update) | async-done | bytes 2097168 | tf_op jit(solution)/shard_map/all_gather | solution.py:32
  109.7 1.8 reduce_sum.27
  111.4 0.2 multiply_reduce_fusion.1
  111.6 0.7 fusion.8
  112.3 2.0 %divide_subtract_fusion.1 = f32[1024,128]{1,0:T(8,128)} fusion(f32[1024,128]{1,0:T(8,128)S(1)} %reduce_sum.27, f32[8192,128]{1,0:T(8,128)} %param.11, s32[]{:T(128)S(6)} %select_n.11, f32[1024]{0:T(1024)S(1)} %get-tuple-element.6), kind=kLoop, calls=%fused_computation.9 | loop fusion | flops 393216 | bytes 1576964 | tf_op jit(solution)/shard_map/sub | solution.py:12
  114.4 0.7 copy.18
  115.1 4.6 %all-to-all-start.1 = ((s32[1,32,1]{2,0,1:T(1,128)}), s32[1,32,1]{2,0,1:T(1,128)S(1)}, u32[]{:S(2)}, u32[]{:S(2)}) async-start(s32[1,32,1]{2,0,1:T(1,128)} %copy.18), calls=%async_computation.2 | async-start | bytes 32768 | tf_op jit(solution)/shard_map/all_to_all | solution.py:48
  119.8 7.0 %all-to-all-done.1 = s32[1,32,1]{2,0,1:T(1,128)S(1)} async-done(((s32[1,32,1]{2,0,1:T(1,128)}), s32[1,32,1]{2,0,1:T(1,128)S(1)}, u32[]{:S(2)}, u32[]{:S(2)}) %all-to-all-start.1) | async-done | bytes 160 | tf_op jit(solution)/shard_map/all_to_all | solution.py:48
  126.8 9.1 %all_to_all.31 = s32[1,32,16]{2,0,1:T(1,128)S(1)} all-to-all(s32[1,32,16]{2,0,1:T(1,128)S(1)} %copy.17), channel_id=1, replica_groups=mesh['rep'=4,'shard'=8] {'rep','shard'}, dimensions={1} | all-to-all | bytes 4096 | tf_op jit(solution)/shard_map/all_to_all | solution.py:47
  135.9 2.6 %all-to-all-start.2 = ((bf16[1,32,16,128]{3,2,0,1:T(8,128)(2,1)}), bf16[1,32,16,128]{3,2,0,1:T(8,128)(2,1)S(1)}, u32[]{:S(2)}, u32[]{:S(2)}) async-start(bf16[1,32,16,128]{3,2,0,1:T(8,128)(2,1)} %bitcast.2), calls=%async_computation.3 | async-start | bytes 262144 | tf_op jit(solution)/shard_map/all_to_all | solution.py:46
  138.5 0.7 reduce.1
  139.3 0.1 lt.33
  139.4 0.5 broadcast.40
  139.9 0.7 reduce.4
  140.7 9.5 %all-to-all-done.2 = bf16[1,32,16,128]{3,2,0,1:T(8,128)(2,1)S(1)} async-done(((bf16[1,32,16,128]{3,2,0,1:T(8,128)(2,1)}), bf16[1,32,16,128]{3,2,0,1:T(8,128)(2,1)S(1)}, u32[]{:S(2)}, u32[]{:S(2)}) %all-to-all-start.2) | async-done | bytes 131104 | tf_op jit(solution)/shard_map/all_to_all | solution.py:46
  150.2 4.6 %scatter_custom_fusion.1 = f32[8192,128]{1,0:T(8,128)} fusion(s32[512]{0:T(512)S(1)} %reshape.77, f32[]{:T(128)} %constant.3.clone.1, bf16[512,128]{1,0:T(8,128)(2,1)S(1)} %bitcast.9, pred[512]{0:T(512)(128)(4,1)S(1)} %lt.33), kind=kCustom, calls=%fused_computation.4 | custom fusion | flops 196608 | bytes 4326912 | tf_op jit(solution)/shard_map/scatter-add | solution.py:56
  154.8 3.5 %multiply_reduce_fusion = f32[8192]{0:T(1024)S(1)} fusion(f32[8192,128]{1,0:T(8,128)} %scatter_custom_fusion.1), kind=kLoop, calls=%fused_computation.3 | loop fusion | flops 2088960 | bytes 4227072 | tf_op jit(solution)/shard_map/reduce_sum | solution.py:11
  158.3 0.6 fusion.7
  158.9 4.2 %divide_subtract_fusion = f32[8192,128]{1,0:T(8,128)} fusion(f32[8192,128]{1,0:T(8,128)} %param.16, f32[8192,128]{1,0:T(8,128)S(1)} %copy-done, f32[8192]{0:T(1024)S(1)} %get-tuple-element.4), kind=kLoop, calls=%fused_computation.2 | loop fusion | flops 3145728 | bytes 12615680 | tf_op jit(solution)/shard_map/sub | solution.py:12
  163.1 14.1 %all_gather.15 = f32[8192]{0:T(1024)S(1)} all-gather(f32[1024]{0:T(1024)S(1)} %get-tuple-element.7), channel_id=1, replica_groups=mesh['rep'=4,'shard'=8] {'shard'}, dimensions={0}, use_global_device_ids=true | all-gather | bytes 36864 | tf_op jit(solution)/shard_map/all_gather | solution.py:43
  177.2 4.5 %copy.22 = f32[8192,128]{1,0:T(8,128)} copy(f32[8192,128]{1,0:T(8,128)} %all-gather.4.cloned.1.call-done) | data formatting | bytes 8388608
  181.7 0.6 copy.23
  (18 shorter events, 0.4 us)
Async XLA Ops:
  7.2 67.0 %reduce-scatter.2.cloned.1.call-start = ((), (), s32[]{:S(2)}) async-start(), calls=%async_computation.4 | async-start | bytes 4718592 | tf_op jit(solution)/shard_map/reduce_scatter | solution.py:29
  21.3 93.1 %copy-start.3 = (s32[1,32]{1,0:T(1,128)S(1)}, s32[1,32]{1,0:T(1,128)}, u32[]{:S(2)}) copy-start(s32[1,32]{1,0:T(1,128)} %param.13) | copy-start | bytes 388
  21.3 98.4 %copy-start.2 = (s32[1,32,16]{1,2,0:T(8,128)S(1)}, s32[1,32,16]{1,2,0:T(8,128)}, u32[]{:S(2)}) copy-start(s32[1,32,16]{1,2,0:T(8,128)} %param.14) | copy-start | bytes 6148
  21.3 88.3 %all-gather.6.cloned.1.call-start = ((), (), s32[]{:S(2)}) async-start(), calls=%async_computation.6 | async-start | bytes 2621440 | tf_op jit(solution)/shard_map/all_gather | solution.py:32
  74.2 103.0 %all-gather.4.cloned.1.call-start = ((), (), s32[]{:S(2)}) async-start(), calls=%async_computation.5 | async-start | bytes 4718592 | tf_op jit(solution)/shard_map/all_gather | solution.py:42
  115.1 11.7 %all-to-all-start.1 = ((s32[1,32,1]{2,0,1:T(1,128)}), s32[1,32,1]{2,0,1:T(1,128)S(1)}, u32[]{:S(2)}, u32[]{:S(2)}) async-start(s32[1,32,1]{2,0,1:T(1,128)} %copy.18), calls=%async_computation.2 | async-start | bytes 32768 | tf_op jit(solution)/shard_map/all_to_all | solution.py:48
  135.9 14.2 %all-to-all-start.2 = ((bf16[1,32,16,128]{3,2,0,1:T(8,128)(2,1)}), bf16[1,32,16,128]{3,2,0,1:T(8,128)(2,1)S(1)}, u32[]{:S(2)}, u32[]{:S(2)}) async-start(bf16[1,32,16,128]{3,2,0,1:T(8,128)(2,1)} %bitcast.2), calls=%async_computation.3 | async-start | bytes 262144 | tf_op jit(solution)/shard_map/all_to_all | solution.py:46
  150.2 8.1 %copy-start.1 = (f32[8192]{0:T(1024)S(1)}, f32[8192]{0:T(1024)}, u32[]{:S(2)}) copy-start(f32[8192]{0:T(1024)} %param.17) | copy-start | bytes 98308
  154.8 4.1 %copy-start = (f32[8192,128]{1,0:T(8,128)S(1)}, f32[8192,128]{1,0:T(8,128)}, u32[]{:S(2)}) copy-start(f32[8192,128]{1,0:T(8,128)} %scatter_custom_fusion.1) | copy-start | bytes 12582916
Sparse Core Ops, SparseCore 0:
  21.4 52.6 reduce-scatter.1
  76.0 33.6 all-gather.5
  114.5 50.0 all-gather.3
